TPU v7x, 128 devices: a whole 4x4x4 slice. The times are simulated.
128 devices in a mesh: img: 16 (over z, y_hi, core), feat: 8 (over y_lo, x).
Axes of the slice: x: 4, y: 4 (y_hi: 2, y_lo: 2; y = y_hi * 2 + y_lo), z: 4, core: 2. Of those that a mesh axis runs over, the one named last changes fastest.
Arguments:
- features: bfloat16 [16384, 32768], P('img', 'feat'), may hold values from -0.055242717 to 0.055242717
- weights: bfloat16 [512, 32768], P('img', 'feat'), may hold values from -20 to 20
- direction: bfloat16 [512, 32768], P('img', 'feat'), may hold values from -6 to 6
Outputs:
- hessian_product: float32 [512, 32768], P('img', 'feat')
All inputs are finite; a program needn't handle non-finite values.
Results may differ from a plain program's by a relative error of at most 0.0024.
Values may be sent and summed in bfloat16 or wider, within the bound.
A program may use at most 64 MiB of HBM per device.

v0:
```python
import jax
import jax.numpy as jnp
from jax import lax
from jax.sharding import PartitionSpec as P


def in_order(parts, dim):
    shape = list(parts.shape[1:])
    shape[dim] *= parts.shape[0]
    return jnp.moveaxis(parts, 0, dim).reshape(shape)


def from_everyone(shard, axis):
    length = lax.axis_size(axis)
    return lax.all_to_all(
        jnp.broadcast_to(shard[None], (length, *shard.shape)), axis, 0, 0, tiled=True
    )


def gathered_copies(shard, axis, dim):
    return in_order(from_everyone(shard, axis), dim)


def weigh(pair):
    prob = jax.nn.sigmoid(pair[0])
    return (prob * (1.0 - prob) * pair[1]).astype(jnp.bfloat16)


def body(features, weights, direction):
    stacked = jnp.stack((weights, direction))
    partial_scores = jnp.einsum(
        "rf,kcf->krc",
        features,
        lax.all_gather(stacked, "img", axis=1, tiled=True),
        preferred_element_type=jnp.float32,
    )
    shares = lax.psum_scatter(partial_scores, "feat", scatter_dimension=1, tiled=True)
    curvature = gathered_copies(weigh(shares), "feat", 0)
    summed_terms = lax.psum_scatter(
        lax.dot_general(
            curvature, features, (((0,), (0,)), ((), ())), preferred_element_type=jnp.float32
        ),
        "img",
        scatter_dimension=0,
        tiled=True,
    )
    return 4.0 * summed_terms


def solution(mesh):
    placed = (P("img", "feat"), P("img", "feat"), P("img", "feat"))
    return jax.shard_map(
        body, mesh=mesh, in_specs=placed, out_specs=P("img", "feat"), check_vma=False
    )
```

profile of v0, /device:TPU:0, one launch (start us, length us, event | category | flops | bytes accessed | tf_op | source)
XLA Modules:
  0.0 291.0 jit_solution(6749987864184155752)
XLA Ops:
  6.5 0.0 all-gather.2.cloned.1.call-start
  6.5 1.9 pad_maximum_fusion
  8.4 0.0 all-gather.2.cloned.1.call-update
  8.4 0.0 reduce-scatter.3.cloned.1.call-start
  8.5 76.7 %all-gather.2.cloned.1.call-done = bf16[2,512,4096]{2,1,0:T(8,128)(2,1)} async-done(((bf16[2,32,4096]{2,1,0:T(8,128)(2,1)}), bf16[2,512,4096]{2,1,0:T(8,128)(2,1)}) %all-gather.2.cloned.1.call-update) | async-done | bytes 8388624 | tf_op jit(solution)/shard_map/all_gather | solution.py:34
  85.2 15.1 %fusion.2 = f32[2,1024,512]{1,2,0:T(8,128)} fusion(bf16[2,512,4096]{2,1,0:T(8,128)(2,1)} %all-gather.2.cloned.1.call-done, bf16[1024,4096]{1,0:T(8,128)(2,1)} %param.3), kind=kOutput, calls=%fused_computation.2 | convolution fusion | flops 8589934592 | bytes 20971520 | tf_op jit(solution)/shard_map/rf,kcf->krc/dot_general | solution.py:31
  100.2 0.0 reduce-scatter.3.cloned.1.call-update
  100.2 0.0 reduce-scatter.5.cloned.1.call-start
  100.3 50.8 %reduce-scatter.3.cloned.1.call-done = f32[2,128,512]{1,2,0:T(8,128)} async-done(((f32[2,1024,512]{1,2,0:T(8,128)}), f32[2,128,512]{1,2,0:T(8,128)}) %reduce-scatter.3.cloned.1.call-update) | async-done | bytes 524304 | tf_op jit(solution)/shard_map/reduce_scatter | solution.py:37
  151.1 1.1 fusion.10
  152.2 0.1 copy.4
  152.4 0.1 broadcast_in_dim.9
  152.5 18.3 %all_to_all.5 = bf16[8,128,512]{2,1,0:T(8,128)(2,1)S(1)} all-to-all(bf16[8,128,512]{2,1,0:T(8,128)(2,1)S(1)} %broadcast_in_dim.9), channel_id=1, replica_groups=mesh['img'=16,'feat'=8] {'feat'}, dimensions={0} | all-to-all | bytes 2097152 | tf_op jit(solution)/shard_map/all_to_all | solution.py:15
  170.8 10.1 %fusion.11 = f32[512,4096]{1,0:T(8,128)} fusion(bf16[1024,512]{1,0:T(8,128)(2,1)S(1)} %bitcast.15, bf16[1024,4096]{1,0:T(8,128)(2,1)} %param.3), kind=kOutput, calls=%fused_computation.13 | convolution fusion | flops 4294967296 | bytes 17825792 | tf_op jit(solution)/shard_map/dot_general | solution.py:40
  180.9 0.0 reduce-scatter.5.cloned.1.call-update
  181.0 101.6 %reduce-scatter.5.cloned.1.call-done = f32[32,4096]{1,0:T(8,128)} async-done(((f32[512,4096]{1,0:T(8,128)}), f32[32,4096]{1,0:T(8,128)}) %reduce-scatter.5.cloned.1.call-update) | async-done | bytes 524304 | tf_op jit(solution)/shard_map/reduce_scatter | solution.py:39
  282.6 1.9 broadcast_multiply_fusion
Async XLA Ops:
  6.5 78.6 %all-gather.2.cloned.1.call-start = ((), (), s32[]{:S(2)}) async-start(), calls=%async_computation.3 | async-start | bytes 8912896 | tf_op jit(solution)/shard_map/all_gather | solution.py:34
  8.4 142.7 %reduce-scatter.3.cloned.1.call-start = ((), (), s32[]{:S(2)}) async-start(), calls=%async_computation.4 | async-start | bytes 4718592 | tf_op jit(solution)/shard_map/reduce_scatter | solution.py:37
  100.2 182.4 %reduce-scatter.5.cloned.1.call-start = ((), (), s32[]{:S(2)}) async-start(), calls=%async_computation.5 | async-start | bytes 8912896 | tf_op jit(solution)/shard_map/reduce_scatter | solution.py:39
Sparse Core Ops, SparseCore 0:
  9.8 75.3 all-gather.1
  100.4 50.7 reduce-scatter.2
  181.1 101.4 reduce-scatter.4
where the time goes:
time: 291 us
  waiting for transfers between devices  229 us (79%)
  matrix products  25.2 us (9%)
  blocking collectives  18.3 us (6%)
  between operations  13.1 us (5%)
  other arithmetic  4.86 us (2%)
    reduce_scatter x1, waiting for transfers between devices, body(): lax.psum_scatter(lax.dot_general(curvature, features, (((0,), (0,)), ((),...  102 us
    all_gather x1, waiting for transfers between devices, body(): lax.all_gather(stacked, 'img', axis=1, tiled=True)  76.7 us
    reduce_scatter x1, waiting for transfers between devices, body(): lax.psum_scatter(partial_scores, 'feat', scatter_dimension=1, tiled=True)  50.8 us
    all_to_all x1, blocking collectives, from_everyone(): lax.all_to_all(jnp.broadcast_to(shard[None], (length, *shard.shape)), axi...  18.3 us
    dot_general x1, matrix products, body(): jnp.einsum('rf,kcf->krc', features, lax.all_gather(stacked, 'img', axis=1...  15.1 us
    dot_general x1, matrix products, body(): lax.dot_general(curvature, features, (((0,), (0,)), ((), ())), preferred_...  10.1 us
  transfers between devices with their start and end apart: 3, of which 3 were waited for; matrix products, arithmetic and copies ran while one was open for 0% of the time, Pallas kernels for 0%

commit v1 on v0

--- a/solution.py
+++ b/solution.py
@@ -31,7 +31,9 @@
     partial_scores = jnp.einsum(
         "rf,kcf->krc",
         features,
-        lax.all_gather(stacked, "img", axis=1, tiled=True),
+        jnp.concatenate(
+            lax.all_to_all(jnp.stack([stacked] * lax.axis_size("img")), "img", 0, 0), axis=1
+        ),
         preferred_element_type=jnp.float32,
     )
     shares = lax.psum_scatter(partial_scores, "feat", scatter_dimension=1, tiled=True)

time: 291 us -> 327 us (1.12)
  blocking collectives: 18.3 us -> 123 us
  waiting for transfers between devices: 229 us -> 152 us
  local copies, waits for them, and re-layouts: 0.2 us -> 8.97 us
    all_to_all x0 -> x1, blocking collectives: none -> 105 us  [body(): lax.all_to_all(jnp.stack([stacked] * lax.axis_size('img')), 'img', 0, 0)]
    all_gather x1 -> x0, waiting for transfers between devices: 76.7 us -> none  [body(): lax.all_gather(stacked, 'img', axis=1, tiled=True)]
    reshape x0 -> x1, local copies, waits for them, and re-layouts: none -> 7.71 us  [body(): jnp.concatenate(lax.all_to_all(jnp.stack([stacked] * lax.axis_size('img')...]
  transfers between devices with their start and end apart: 3 -> 2, of which waited for: 3 -> 2; matrix products, arithmetic and copies ran while one was open for 0% -> 0% of each run, Pallas kernels for 0% -> 0%
where the time goes in v1:
time: 327 us; the launch traced here: 326 us
  waiting for transfers between devices  152 us (46%)
  blocking collectives  123 us (38%)
  matrix products  25.2 us (8%)
  between operations  13.4 us (4%)
  local copies, waits for them, and re-layouts  8.97 us (3%)
  other arithmetic  4.07 us (1%)
    all_to_all x1, blocking collectives, body(): lax.all_to_all(jnp.stack([stacked] * lax.axis_size('img')), 'img', 0, 0)  105 us
    reduce_scatter x1, waiting for transfers between devices, body(): lax.psum_scatter(lax.dot_general(curvature, features, (((0,), (0,)), ((),...  102 us
    reduce_scatter x1, waiting for transfers between devices, body(): lax.psum_scatter(partial_scores, 'feat', scatter_dimension=1, tiled=True)  50 us
    all_to_all x1, blocking collectives, from_everyone(): lax.all_to_all(jnp.broadcast_to(shard[None], (length, *shard.shape)), axi...  18.4 us
    dot_general x1, matrix products, body(): jnp.einsum('rf,kcf->krc', features, jnp.concatenate(lax.all_to_all(jnp.st...  15.1 us
    dot_general x1, matrix products, body(): lax.dot_general(curvature, features, (((0,), (0,)), ((), ())), preferred_...  10.1 us
    reshape x1, local copies, waits for them, and re-layouts, body(): jnp.concatenate(lax.all_to_all(jnp.stack([stacked] * lax.axis_size('img')...  7.71 us
  transfers between devices with their start and end apart: 2, of which 2 were waited for; matrix products, arithmetic and copies ran while one was open for 0% of the time, Pallas kernels for 0%

profile of v1, /device:TPU:0, one launch (start us, length us, event | category | flops | bytes accessed | tf_op | source)
XLA Modules:
  0.0 326.5 jit_solution(10309177773046937133)
XLA Ops:
  6.5 0.0 reduce-scatter.3.cloned.1.call-start
  6.5 1.1 pad_maximum_fusion
  7.6 1.1 stack.11
  8.7 104.7 %all_to_all.10 = bf16[16,2,32,4096]{3,2,1,0:T(8,128)(2,1)} all-to-all(bf16[16,2,32,4096]{3,2,1,0:T(8,128)(2,1)S(1)} %stack.11), channel_id=1, replica_groups=mesh['img'=16,'feat'=8] {'img'}, dimensions={0} | all-to-all | bytes 16777216 | tf_op jit(solution)/shard_map/all_to_all | solution.py:35
  113.4 7.7 %copy.5 = bf16[2,16,32,4096]{3,2,1,0:T(8,128)(2,1)} copy(bf16[2,16,32,4096]{3,2,0,1:T(8,128)(2,1)} %bitcast.17) | data formatting | bytes 16777216 | tf_op jit(solution)/shard_map/reshape | solution.py:34
  121.1 15.1 %fusion.2 = f32[2,1024,512]{1,2,0:T(8,128)} fusion(bf16[2,512,4096]{2,1,0:T(8,128)(2,1)} %bitcast.18, bf16[1024,4096]{1,0:T(8,128)(2,1)} %param.3), kind=kOutput, calls=%fused_computation.2 | convolution fusion | flops 8589934592 | bytes 20971520 | tf_op jit(solution)/shard_map/rf,kcf->krc/dot_general | solution.py:31
  136.1 0.0 reduce-scatter.3.cloned.1.call-update
  136.2 0.0 reduce-scatter.5.cloned.1.call-start
  136.2 50.0 %reduce-scatter.3.cloned.1.call-done = f32[2,128,512]{1,2,0:T(8,128)} async-done(((f32[2,1024,512]{1,2,0:T(8,128)}), f32[2,128,512]{1,2,0:T(8,128)}) %reduce-scatter.3.cloned.1.call-update) | async-done | bytes 524304 | tf_op jit(solution)/shard_map/reduce_scatter | solution.py:39
  186.2 1.1 fusion.10
  187.3 0.1 copy.6
  187.4 0.1 broadcast_in_dim.9
  187.5 18.4 %all_to_all.11 = bf16[8,128,512]{2,1,0:T(8,128)(2,1)S(1)} all-to-all(bf16[8,128,512]{2,1,0:T(8,128)(2,1)S(1)} %broadcast_in_dim.9), channel_id=1, replica_groups=mesh['img'=16,'feat'=8] {'feat'}, dimensions={0} | all-to-all | bytes 2097152 | tf_op jit(solution)/shard_map/all_to_all | solution.py:15
  205.9 10.1 %fusion.11 = f32[512,4096]{1,0:T(8,128)} fusion(bf16[1024,512]{1,0:T(8,128)(2,1)S(1)} %bitcast.19, bf16[1024,4096]{1,0:T(8,128)(2,1)} %param.3), kind=kOutput, calls=%fused_computation.13 | convolution fusion | flops 4294967296 | bytes 17825792 | tf_op jit(solution)/shard_map/dot_general | solution.py:42
  216.0 0.0 reduce-scatter.5.cloned.1.call-update
  216.0 101.7 %reduce-scatter.5.cloned.1.call-done = f32[32,4096]{1,0:T(8,128)} async-done(((f32[512,4096]{1,0:T(8,128)}), f32[32,4096]{1,0:T(8,128)}) %reduce-scatter.5.cloned.1.call-update) | async-done | bytes 524304 | tf_op jit(solution)/shard_map/reduce_scatter | solution.py:41
  317.7 1.9 broadcast_multiply_fusion
Async XLA Ops:
  6.5 179.6 %reduce-scatter.3.cloned.1.call-start = ((), (), s32[]{:S(2)}) async-start(), calls=%async_computation.4 | async-start | bytes 4718592 | tf_op jit(solution)/shard_map/reduce_scatter | solution.py:39
  136.2 181.6 %reduce-scatter.5.cloned.1.call-start = ((), (), s32[]{:S(2)}) async-start(), calls=%async_computation.5 | async-start | bytes 8912896 | tf_op jit(solution)/shard_map/reduce_scatter | solution.py:41
Sparse Core Ops, SparseCore 0:
  136.3 49.8 reduce-scatter.2
  216.2 101.5 reduce-scatter.4
